TPU v7x, 128 devices: a whole 4x4x4 slice. The times are simulated.
128 devices in a mesh: gx: 4 (over z), gy: 4 (over y), gz: 8 (over x, core).
Axes of the slice: x: 4, y: 4, z: 4, core: 2. Of those that a mesh axis runs over, the one named last changes fastest.
Arguments:
- interact: bfloat16 [16, 32768, 512], P(None, ('gx', 'gy', 'gz')), may hold values from -6 to 6
- weight_one: bfloat16 [512, 1024], replicated, may hold values from -0.25 to 0.25
- bias_one: float32 [1024], replicated, may hold values from -3 to 3
- weight_two: bfloat16 [1024, 1024], replicated, may hold values from -0.1875 to 0.1875
- bias_two: float32 [1024], replicated, may hold values from -3 to 3
- weight_three: bfloat16 [1024, 512], replicated, may hold values from -0.1875 to 0.1875
- bias_three: float32 [512], replicated, may hold values from -3 to 3
- weight_four: bfloat16 [512, 256], replicated, may hold values from -0.25 to 0.25
- bias_four: float32 [256], replicated, may hold values from -3 to 3
- weight_out: bfloat16 [256, 1], replicated, may hold values from -1 to 1
- bias_out: float32 [1], replicated, may hold values from -1.5 to 0
- bucket_index: int32 [16, 32768], P(None, ('gx', 'gy', 'gz')), may hold values from 0 to 4095
- labels: int32 [16, 32768], P(None, ('gx', 'gy', 'gz')), may hold values from 0 to 1
Outputs:
- bucket_stats: float32 [16, 4, 4096], P(None, None, 'gx')
- summary: float32 [16, 4], replicated
All inputs are finite; a program needn't handle non-finite values.
Results may differ from a plain program's by a relative error of at most 0.0045.
Values sent between devices are 32-bit elements; how exact they have to be, the bound alone decides.
No kernel may reach another device: no remote copies, remote signals or barrier semaphores. Data moves between devices by JAX's collectives and lax.ppermute only.
A program may use at most 128 MiB of HBM per device.

v0:
```python
import jax
import jax.numpy as jnp
from jax import lax
from jax.sharding import PartitionSpec as P

NBUCK = 4096


def split_up(value, dim, size):
    before, after = (value.shape[:dim], value.shape[dim + 1 :])
    return jnp.moveaxis(value.reshape(*before, size, -1, *after), dim, 0)


def sent_and_summed(value, axis, dim):
    tiles = split_up(value, dim, lax.axis_size(axis))
    arrived = lax.all_to_all(tiles, axis, split_axis=0, concat_axis=0, tiled=True)
    return arrived.sum(axis=0)


def gathered_total(value, axis):
    tiles = lax.all_gather(value, axis)
    return tiles.sum(axis=0)


def from_everyone(value, axis):
    size = lax.axis_size(axis)
    return lax.all_to_all(
        jnp.broadcast_to(value[None], (size, *value.shape)), axis, 0, 0, tiled=True
    )


def folded_in_pairs(pieces, combine):
    while len(jax.tree.leaves(pieces)[0]) > 1:
        pieces = jax.vmap(combine)(*(pieces[side::2] for side in (0, 1)))
    return pieces[0]


def carried_in(value, axis, combine, identity):
    size, index = (lax.axis_size(axis), lax.axis_index(axis))
    passed = jnp.arange(size) < index

    def kept(part, zero, own):
        part = jnp.where(
            passed.reshape(-1, *(1 for _ in own.shape)), part, jnp.asarray(zero, own.dtype)
        )
        return part

    pieces = from_everyone(value, axis)
    return folded_in_pairs(kept(pieces, identity, value), combine)


def one_axis_at_a_time(value, axes):
    for axis in axes:
        value = lax.psum(value, axis)
    return value


def joined_along(tiles, dim):
    shape = list(tiles.shape[1:])
    shape[dim] *= tiles.shape[0]
    return jnp.moveaxis(tiles, 0, dim).reshape(shape)


def gather_directly(value, axis, dim):
    tiles = from_everyone(value, axis)
    return joined_along(tiles, dim)


def layer_relu(inputs, weight, offset):
    return jax.nn.relu(jnp.dot(inputs, weight, preferred_element_type=jnp.float32) + offset).astype(
        jnp.bfloat16
    )


def bucket_reports(totals):
    positives = totals[:, 0]
    negatives = totals[:, 1]
    counts = jnp.maximum(positives + negatives, 1.0)
    return jnp.stack(
        [positives / counts, totals[:, 2] / counts, totals[:, 3] / counts, totals[:, 4] / counts],
        axis=1,
    )


def summarize(numerator, column_sums):
    pair_count = jnp.maximum(column_sums[:, 0] * column_sums[:, 1], 1.0)
    example_count = jnp.maximum(column_sums[:, 0] + column_sums[:, 1], 1.0)
    return jnp.stack(
        [
            numerator / pair_count,
            column_sums[:, 3] / example_count,
            column_sums[:, 2] / jnp.maximum(column_sums[:, 0], 1.0),
            column_sums[:, 4] / example_count,
        ],
        axis=1,
    )


def combine_add(earlier, later):
    return earlier + later


def split_parts(values):
    upper = values.astype(jnp.bfloat16)
    remain = values - upper.astype(jnp.float32)
    middle = remain.astype(jnp.bfloat16)
    lower = (remain - middle.astype(jnp.float32)).astype(jnp.bfloat16)
    return jnp.concatenate([upper, middle, lower], axis=0)


def merge_reports(histograms):
    bucket_share = sent_and_summed(histograms, ("gx", "gy"), 2)
    bucket_share = gathered_total(bucket_share, "gz")
    reports = bucket_reports(bucket_share)
    negatives = bucket_share[:, 1]
    negative_sums = jnp.sum(negatives, axis=1)
    before = carried_in(negative_sums, ("gx", "gy"), combine_add, jnp.zeros_like(negative_sums))
    below_count = before[:, None] + jnp.cumsum(negatives, axis=1) - negatives
    partial_numerator = jnp.sum(bucket_share[:, 0] * (below_count + 0.5 * negatives), axis=1)
    numerator, column_sums = (
        one_axis_at_a_time(partial_numerator, ("gx", "gy")),
        one_axis_at_a_time(jnp.sum(bucket_share, axis=2), ("gx", "gy")),
    )
    report_block = gather_directly(reports, "gy", 2)
    return (report_block, summarize(numerator, column_sums))


def on_device(
    interact,
    weight_one,
    bias_one,
    weight_two,
    bias_two,
    weight_three,
    bias_three,
    weight_four,
    bias_four,
    weight_out,
    bias_out,
    bucket_index,
    labels,
):
    intervals, local_rows, features_in = interact.shape
    flat_rows = interact.reshape(intervals * local_rows, features_in)
    hidden = layer_relu(flat_rows, weight_one, bias_one)
    hidden = layer_relu(hidden, weight_two, bias_two)
    hidden = layer_relu(hidden, weight_three, bias_three)
    hidden = layer_relu(hidden, weight_four, bias_four)
    logits = jnp.dot(hidden, weight_out, preferred_element_type=jnp.float32)[:, 0] + bias_out[0]
    logits = logits.reshape(intervals, local_rows)
    observed = labels.astype(jnp.float32)
    predicted = jax.nn.sigmoid(logits)
    losses = jax.nn.softplus(logits) - observed * logits
    squared = (predicted - observed) ** 2
    values = jnp.stack([observed, 1.0 - observed, predicted, losses, squared], axis=1)
    bucket_ids = lax.broadcasted_iota(jnp.int32, (1, NBUCK), 1)

    def histogram_one(inputs):
        row_values, buckets = inputs
        one_hot = (buckets[:, None] == bucket_ids).astype(jnp.bfloat16)
        parts = split_parts(row_values)
        partial_value = jnp.dot(parts, one_hot, preferred_element_type=jnp.float32)
        return jnp.sum(partial_value.reshape(3, row_values.shape[0], NBUCK), axis=0)

    histograms = lax.map(histogram_one, (values, bucket_index))
    bucket_stats, summary = merge_reports(histograms)
    return (bucket_stats, summary)


def solution(mesh):
    in_specs = (
        P(None, ("gx", "gy", "gz"), None),
        P(),
        P(),
        P(),
        P(),
        P(),
        P(),
        P(),
        P(),
        P(),
        P(),
        P(None, ("gx", "gy", "gz")),
        P(None, ("gx", "gy", "gz")),
    )
    out_specs = (P(None, None, "gx"), P())
    return jax.shard_map(
        on_device, mesh=mesh, in_specs=in_specs, out_specs=out_specs, check_vma=False
    )
```

profile of v0, /device:TPU:0, one launch (start us, length us, event | category | flops | bytes accessed | tf_op | source)
XLA Modules:
  0.0 154.5 jit_solution(18154456367741899383)
XLA Ops:
  1.4 0.8 copy-done
  2.3 18.6 %fusion.11 = f32[4096,1024]{1,0:T(8,128)} fusion(bf16[1024,1024]{1,0:T(8,128)(2,1)S(1)} %copy-done, f32[1024]{0:T(1024)} %param.17, bf16[4096,512]{1,0:T(8,128)(2,1)} %bitcast.83, bf16[512,1024]{1,0:T(8,128)(2,1)} %param.16), kind=kOutput, calls=%fused_computation.18 | convolution fusion | flops 12897484800 | bytes 24121344 | tf_op jit(solution)/shard_map/dot_general | solution.py:70
  20.9 10.5 %fusion.20 = bf16[4096,256]{1,0:T(8,128)(2,1)} fusion(bf16[512,256]{1,0:T(8,128)(2,1)S(1)} %copy-done.4, bf16[1024,512]{1,0:T(8,128)(2,1)S(1)} %copy-done.3, f32[4096,1024]{1,0:T(8,128)} %fusion.11, f32[1024]{0:T(1024)S(1)} %copy-done.5, f32[512]{0:T(512)S(1)} %copy-done.6, f32[256]{0:T(256)S(1)} %copy-done.7), kind=kOutput, calls=%fused_computation.28 | convolution fusion | flops 5390729216 | bytes 20192256 | tf_op jit(solution)/shard_map/dot_general | solution.py:70
  31.4 2.2 %fusion.34 = f32[1,4096]{1,0:T(1,128)S(1)} fusion(bf16[4096,256]{1,0:T(8,128)(2,1)} %fusion.20, bf16[256,1]{0,1:T(2,128)(2,1)S(1)} %copy-done.2), kind=kOutput, calls=%fused_computation.66 | convolution fusion | flops 2097152 | bytes 2114048 | tf_op jit(solution)/shard_map/dot_general | solution.py:149
  34.0 36.2 %while.11 = (s32[]{:T(128)}, f32[16,5,4096]{2,1,0:T(8,128)}, f32[16,5,256]{2,1,0:T(8,128)S(1)}, s32[16,256]{1,0:T(8,128)}, s32[]{:T(128)}, /*index=5*/f32[]{:T(128)}) while((s32[]{:T(128)}, f32[16,5,4096]{2,1,0:T(8,128)}, f32[16,5,256]{2,1,0:T(8,128)S(1)}, s32[16,256]{1,0:T(8,128)}, s32[]{:T(128)}, /*index=5*/f32[]{:T(128)}) %tuple.41), condition=%wide.region_2.3_spmd.clone, body=%wide.region_0.2_spmd.clone.sunk | while | flops 32577536 | bytes 1304657 | solution.py:165
  34.0 0.7 constant_dynamic-slice_fusion.2
  34.7 0.8 fusion.45
  36.3 0.7 constant_dynamic-slice_fusion.2
  37.0 0.8 fusion.45
  38.5 0.7 constant_dynamic-slice_fusion.2
  39.2 0.8 fusion.45
  40.8 0.7 constant_dynamic-slice_fusion.2
  41.5 0.8 fusion.45
  43.1 0.7 constant_dynamic-slice_fusion.2
  43.8 0.8 fusion.45
  45.3 0.7 constant_dynamic-slice_fusion.2
  46.0 0.8 fusion.45
  47.6 0.7 constant_dynamic-slice_fusion.2
  48.3 0.8 fusion.45
  49.8 0.7 constant_dynamic-slice_fusion.2
  50.5 0.8 fusion.45
  52.1 0.7 constant_dynamic-slice_fusion.2
  52.8 0.8 fusion.45
  54.4 0.7 constant_dynamic-slice_fusion.2
  55.1 0.8 fusion.45
  56.6 0.7 constant_dynamic-slice_fusion.2
  57.3 0.8 fusion.45
  58.9 0.7 constant_dynamic-slice_fusion.2
  59.6 0.8 fusion.45
  61.1 0.7 constant_dynamic-slice_fusion.2
  61.8 0.8 fusion.45
  64.1 0.8 fusion.45
  65.7 0.7 constant_dynamic-slice_fusion.2
  66.4 0.8 fusion.45
  67.9 0.7 constant_dynamic-slice_fusion.2
  68.6 0.8 fusion.45
  70.2 2.0 %reshape.100 = f32[16,5,16,256]{3,2,1,0:T(8,128)S(1)} reshape(f32[16,5,4096]{2,1,0:T(8,128)} %get-tuple-element.29) | data formatting | bytes 2621440 | tf_op jit(solution)/shard_map/reshape | solution.py:11
  72.2 1.8 %copy.54 = f32[16,16,5,256]{3,1,2,0:T(8,128)} copy(f32[16,16,5,256]{3,0,2,1:T(8,128)S(1)} %bitcast.76) | data formatting | bytes 2621440 | tf_op jit(solution)/shard_map/transpose | solution.py:11
  74.0 8.2 %all-to-all-start = ((f32[16,16,5,256]{3,1,2,0:T(8,128)}), f32[16,16,5,256]{3,1,2,0:T(8,128)S(1)}, u32[]{:S(2)}, u32[]{:S(2)}) async-start(f32[16,16,5,256]{3,1,2,0:T(8,128)} %copy.54), calls=%async_computation | async-start | bytes 2621440 | tf_op jit(solution)/shard_map/all_to_all | solution.py:16
  82.2 20.9 %all-to-all-done = f32[16,16,5,256]{3,1,2,0:T(8,128)S(1)} async-done(((f32[16,16,5,256]{3,1,2,0:T(8,128)}), f32[16,16,5,256]{3,1,2,0:T(8,128)S(1)}, u32[]{:S(2)}, u32[]{:S(2)}) %all-to-all-start) | async-done | bytes 1310752 | tf_op jit(solution)/shard_map/all_to_all | solution.py:16
  103.2 13.6 %all-gather = f32[128,5,256]{2,0,1:T(8,128)S(1)} all-gather(f32[16,5,256]{2,0,1:T(8,128)S(1)} %reduce_sum.54), channel_id=2, replica_groups=mesh['gx'=4,'gy'=4,'gz'=8] {'gz'}, dimensions={0}, use_global_device_ids=true | all-gather | bytes 737280 | tf_op jit(solution)/shard_map/all_gather | solution.py:21
  117.6 3.5 %all-to-all-start.2 = ((f32[16,1,16]{2,1,0:T(1,128)}), f32[16,1,16]{2,1,0:T(1,128)S(1)}, u32[]{:S(2)}, u32[]{:S(2)}) async-start(f32[16,1,16]{2,1,0:T(1,128)} %broadcast_in_dim.39), calls=%async_computation.2 | async-start | bytes 16384 | tf_op jit(solution)/shard_map/all_to_all | solution.py:27
  122.3 6.3 %all-to-all-done.2 = f32[16,1,16]{2,1,0:T(1,128)S(1)} async-done(((f32[16,1,16]{2,1,0:T(1,128)}), f32[16,1,16]{2,1,0:T(1,128)S(1)}, u32[]{:S(2)}, u32[]{:S(2)}) %all-to-all-start.2) | async-done | bytes 1056 | tf_op jit(solution)/shard_map/all_to_all | solution.py:27
  128.5 0.7 broadcast_in_dim.24
  129.3 3.4 %all-to-all-start.1 = ((f32[4,16,4,256]{3,2,1,0:T(4,128)}), f32[4,16,4,256]{3,2,1,0:T(4,128)S(1)}, u32[]{:S(2)}, u32[]{:S(2)}) async-start(f32[4,16,4,256]{3,2,1,0:T(4,128)} %broadcast_in_dim.24), calls=%async_computation.1 | async-start | bytes 524288 | tf_op jit(solution)/shard_map/all_to_all | solution.py:27
  133.1 9.0 %all-reduce.1 = (f32[16,5]{0,1:T(8,128)S(1)}, f32[16]{0:T(128)S(1)}) all-reduce(f32[16,5]{0,1:T(8,128)S(1)} %reduce_sum.58, f32[16]{0:T(128)S(1)} %fusion.28), channel_id=1, replica_groups=mesh['gx'=4,'gy'=4,'gz'=8] {'gx'}, use_global_device_ids=true, to_apply=%region_12.13 | all-reduce | flops 96 | bytes 768 | tf_op jit(solution)/shard_map/psum | solution.py:54
  142.1 11.0 %all-reduce = (f32[16,5]{0,1:T(8,128)S(1)}, f32[16]{0:T(128)S(1)}) all-reduce(f32[16,5]{0,1:T(8,128)S(1)} %get-tuple-element.54, f32[16]{0:T(128)S(1)} %get-tuple-element.55), channel_id=1, replica_groups=mesh['gx'=4,'gy'=4,'gz'=8] {'gy'}, use_global_device_ids=true, to_apply=%region_13.14 | all-reduce | flops 96 | bytes 768 | tf_op jit(solution)/shard_map/psum | solution.py:54
  153.8 0.7 copy.66
  (123 shorter events, 15.9 us)
Async XLA Ops:
  0.6 1.6 %copy-start = (bf16[1024,1024]{1,0:T(8,128)(2,1)S(1)}, bf16[1024,1024]{1,0:T(8,128)(2,1)}, u32[]{:S(2)}) copy-start(bf16[1024,1024]{1,0:T(8,128)(2,1)} %param.18) | copy-start | bytes 6291460
  2.2 18.6 %copy-start.3 = (bf16[1024,512]{1,0:T(8,128)(2,1)S(1)}, bf16[1024,512]{1,0:T(8,128)(2,1)}, u32[]{:S(2)}) copy-start(bf16[1024,512]{1,0:T(8,128)(2,1)} %param.20) | copy-start | bytes 3145732
  2.2 18.6 %copy-start.4 = (bf16[512,256]{1,0:T(8,128)(2,1)S(1)}, bf16[512,256]{1,0:T(8,128)(2,1)}, u32[]{:S(2)}) copy-start(bf16[512,256]{1,0:T(8,128)(2,1)} %param.22) | copy-start | bytes 786436
  2.2 18.6 %copy-start.5 = (f32[1024]{0:T(1024)S(1)}, f32[1024]{0:T(1024)}, u32[]{:S(2)}) copy-start(f32[1024]{0:T(1024)} %param.19) | copy-start | bytes 12292
  2.2 18.6 %copy-start.6 = (f32[512]{0:T(512)S(1)}, f32[512]{0:T(512)}, u32[]{:S(2)}) copy-start(f32[512]{0:T(512)} %param.21) | copy-start | bytes 6148
  2.3 18.6 %copy-start.7 = (f32[256]{0:T(256)S(1)}, f32[256]{0:T(256)}, u32[]{:S(2)}) copy-start(f32[256]{0:T(256)} %param.23) | copy-start | bytes 3076
  20.9 10.5 %copy-start.2 = (bf16[256,1]{0,1:T(2,128)(2,1)S(1)}, bf16[256,1]{0,1:T(2,128)(2,1)}, u32[]{:S(2)}) copy-start(bf16[256,1]{0,1:T(2,128)(2,1)} %param.24) | copy-start | bytes 1540
  20.9 12.8 %copy-start.1 = (s32[16,256]{1,0:T(8,128)S(1)}, s32[16,256]{1,0:T(8,128)}, u32[]{:S(2)}) copy-start(s32[16,256]{1,0:T(8,128)} %param.27) | copy-start | bytes 49156
  74.0 29.1 %all-to-all-start = ((f32[16,16,5,256]{3,1,2,0:T(8,128)}), f32[16,16,5,256]{3,1,2,0:T(8,128)S(1)}, u32[]{:S(2)}, u32[]{:S(2)}) async-start(f32[16,16,5,256]{3,1,2,0:T(8,128)} %copy.54), calls=%async_computation | async-start | bytes 2621440 | tf_op jit(solution)/shard_map/all_to_all | solution.py:16
  117.6 10.9 %all-to-all-start.2 = ((f32[16,1,16]{2,1,0:T(1,128)}), f32[16,1,16]{2,1,0:T(1,128)S(1)}, u32[]{:S(2)}, u32[]{:S(2)}) async-start(f32[16,1,16]{2,1,0:T(1,128)} %broadcast_in_dim.39), calls=%async_computation.2 | async-start | bytes 16384 | tf_op jit(solution)/shard_map/all_to_all | solution.py:27
  129.3 24.5 %all-to-all-start.1 = ((f32[4,16,4,256]{3,2,1,0:T(4,128)}), f32[4,16,4,256]{3,2,1,0:T(4,128)S(1)}, u32[]{:S(2)}, u32[]{:S(2)}) async-start(f32[4,16,4,256]{3,2,1,0:T(4,128)} %broadcast_in_dim.24), calls=%async_computation.1 | async-start | bytes 524288 | tf_op jit(solution)/shard_map/all_to_all | solution.py:27
where the time goes:
time: 156 us; the launch traced here: 154 us
  matrix products  44.1 us (28%)
  blocking collectives  33.6 us (22%)
  local copies, waits for them, and re-layouts  29.8 us (19%)
  waiting for transfers between devices  27.2 us (17%)
  starting transfers between devices  15 us (10%)
  other arithmetic  2.68 us (2%)
  between operations  1.7 us (1%)
    dot_general x2, matrix products, layer_relu(): jnp.dot(inputs, weight, preferred_element_type=jnp.float32) + offset  29.1 us
    all_to_all x1, waiting for transfers between devices, sent_and_summed(): lax.all_to_all(tiles, axis, split_axis=0, concat_axis=0, tiled=True)  20.9 us
    psum x2, blocking collectives, one_axis_at_a_time(): value = lax.psum(value, axis)  20 us
    all_gather x1, blocking collectives, gathered_total(): tiles = lax.all_gather(value, axis)  13.6 us
    dot_general x16, matrix products, histogram_one(): partial_value = jnp.dot(parts, one_hot, preferred_element_type=jnp.float32)  12.8 us
    dynamic_slice x16, local copies, waits for them, and re-layouts, on_device(): histograms = lax.map(histogram_one, (values, bucket_index))  11.2 us
    dynamic_update_slice x16, local copies, waits for them, and re-layouts, on_device(): histograms = lax.map(histogram_one, (values, bucket_index))  10.6 us
    all_to_all x1, starting transfers between devices, sent_and_summed(): lax.all_to_all(tiles, axis, split_axis=0, concat_axis=0, tiled=True)  8.16 us
  transfers between devices with their start and end apart: 3, of which 2 were waited for; matrix products, arithmetic and copies ran while one was open for 1% of the time, Pallas kernels for 0%

commit v1 on v0

--- a/solution.py
+++ b/solution.py
@@ -51,7 +51,7 @@
 
 def one_axis_at_a_time(value, axes):
     for axis in axes:
-        value = lax.psum(value, axis)
+        value = jnp.sum(lax.all_gather(value, axis), axis=0)
     return value
 
 

time: 156 us -> 177 us (1.13)
  blocking collectives: 33.6 us -> 59.6 us
  waiting for transfers between devices: 27.2 us -> 18.4 us
  local copies, waits for them, and re-layouts: 29.8 us -> 31.7 us
    all_gather x0 -> x2, blocking collectives: none -> 25 us  [one_axis_at_a_time(): value = jnp.sum(lax.all_gather(value, axis), axis=0)]
    unnamed x0 -> x2, blocking collectives: none -> 21 us
    psum x2 -> x0, blocking collectives: 20 us -> none  [one_axis_at_a_time(): value = lax.psum(value, axis)]
    all_to_all x2, waiting for transfers between devices: 6.27 us -> 0.01 us  [from_everyone(): lax.all_to_all(jnp.broadcast_to(value[None], (size, *value.shape)), axis,...]
    all_to_all x1, waiting for transfers between devices: 20.9 us -> 18.4 us  [sent_and_summed(): lax.all_to_all(tiles, axis, split_axis=0, concat_axis=0, tiled=True)]
  transfers between devices with their start and end apart: 3 -> 3, of which waited for: 2 -> 1; matrix products, arithmetic and copies ran while one was open for 1% -> 2% of each run, Pallas kernels for 0% -> 0%
where the time goes in v1:
time: 177 us; the launch traced here: 175 us
  blocking collectives  59.6 us (34%)
  matrix products  44.1 us (25%)
  local copies, waits for them, and re-layouts  31.7 us (18%)
  waiting for transfers between devices  18.4 us (10%)
  starting transfers between devices  15.3 us (9%)
  between operations  3 us (2%)
  other arithmetic  2.75 us (2%)
    dot_general x2, matrix products, layer_relu(): jnp.dot(inputs, weight, preferred_element_type=jnp.float32) + offset  29.1 us
    all_gather x2, blocking collectives, one_axis_at_a_time(): value = jnp.sum(lax.all_gather(value, axis), axis=0)  25 us
    unnamed x2, blocking collectives  21 us
    all_to_all x1, waiting for transfers between devices, sent_and_summed(): lax.all_to_all(tiles, axis, split_axis=0, concat_axis=0, tiled=True)  18.4 us
    all_gather x1, blocking collectives, gathered_total(): tiles = lax.all_gather(value, axis)  13.6 us
    dot_general x16, matrix products, histogram_one(): partial_value = jnp.dot(parts, one_hot, preferred_element_type=jnp.float32)  12.8 us
    dynamic_slice x16, local copies, waits for them, and re-layouts, on_device(): histograms = lax.map(histogram_one, (values, bucket_index))  11.2 us
    dynamic_update_slice x16, local copies, waits for them, and re-layouts, on_device(): histograms = lax.map(histogram_one, (values, bucket_index))  10.6 us
  transfers between devices with their start and end apart: 3, of which 1 were waited for; matrix products, arithmetic and copies ran while one was open for 2% of the time, Pallas kernels for 0%

profile of v1, /device:TPU:0, one launch (start us, length us, event | category | flops | bytes accessed | tf_op | source)
XLA Modules:
  0.0 175.2 jit_solution(15671276114538975145)
XLA Ops:
  1.4 0.8 copy-done
  2.3 18.6 %fusion.11 = f32[4096,1024]{1,0:T(8,128)} fusion(bf16[1024,1024]{1,0:T(8,128)(2,1)S(1)} %copy-done, f32[1024]{0:T(1024)} %param.17, bf16[4096,512]{1,0:T(8,128)(2,1)} %bitcast.85, bf16[512,1024]{1,0:T(8,128)(2,1)} %param.16), kind=kOutput, calls=%fused_computation.18 | convolution fusion | flops 12897484800 | bytes 24121344 | tf_op jit(solution)/shard_map/dot_general | solution.py:70
  20.9 10.5 %fusion.20 = bf16[4096,256]{1,0:T(8,128)(2,1)} fusion(bf16[512,256]{1,0:T(8,128)(2,1)S(1)} %copy-done.4, bf16[1024,512]{1,0:T(8,128)(2,1)S(1)} %copy-done.3, f32[4096,1024]{1,0:T(8,128)} %fusion.11, f32[1024]{0:T(1024)S(1)} %copy-done.5, f32[512]{0:T(512)S(1)} %copy-done.6, f32[256]{0:T(256)S(1)} %copy-done.7), kind=kOutput, calls=%fused_computation.28 | convolution fusion | flops 5390729216 | bytes 20192256 | tf_op jit(solution)/shard_map/dot_general | solution.py:70
  31.4 2.2 %fusion.33 = f32[1,4096]{1,0:T(1,128)S(1)} fusion(bf16[4096,256]{1,0:T(8,128)(2,1)} %fusion.20, bf16[256,1]{0,1:T(2,128)(2,1)S(1)} %copy-done.2), kind=kOutput, calls=%fused_computation.65 | convolution fusion | flops 2097152 | bytes 2114048 | tf_op jit(solution)/shard_map/dot_general | solution.py:149
  34.0 36.2 %while.11 = (s32[]{:T(128)}, f32[16,5,4096]{2,1,0:T(8,128)}, f32[16,5,256]{2,1,0:T(8,128)S(1)}, s32[16,256]{1,0:T(8,128)}, s32[]{:T(128)}, /*index=5*/f32[]{:T(128)}) while((s32[]{:T(128)}, f32[16,5,4096]{2,1,0:T(8,128)}, f32[16,5,256]{2,1,0:T(8,128)S(1)}, s32[16,256]{1,0:T(8,128)}, s32[]{:T(128)}, /*index=5*/f32[]{:T(128)}) %tuple.42), condition=%wide.region_2.3_spmd.clone, body=%wide.region_0.2_spmd.clone.sunk | while | flops 32577536 | bytes 1304657 | solution.py:165
  34.0 0.7 constant_dynamic-slice_fusion.2
  34.7 0.8 fusion.44
  36.3 0.7 constant_dynamic-slice_fusion.2
  37.0 0.8 fusion.44
  38.5 0.7 constant_dynamic-slice_fusion.2
  39.2 0.8 fusion.44
  40.8 0.7 constant_dynamic-slice_fusion.2
  41.5 0.8 fusion.44
  43.1 0.7 constant_dynamic-slice_fusion.2
  43.8 0.8 fusion.44
  45.3 0.7 constant_dynamic-slice_fusion.2
  46.0 0.8 fusion.44
  47.6 0.7 constant_dynamic-slice_fusion.2
  48.3 0.8 fusion.44
  49.8 0.7 constant_dynamic-slice_fusion.2
  50.5 0.8 fusion.44
  52.1 0.7 constant_dynamic-slice_fusion.2
  52.8 0.8 fusion.44
  54.4 0.7 constant_dynamic-slice_fusion.2
  55.1 0.8 fusion.44
  56.6 0.7 constant_dynamic-slice_fusion.2
  57.3 0.8 fusion.44
  58.9 0.7 constant_dynamic-slice_fusion.2
  59.6 0.8 fusion.44
  61.9 0.8 fusion.44
  63.4 0.7 constant_dynamic-slice_fusion.2
  64.1 0.8 fusion.44
  66.4 0.8 fusion.44
  67.9 0.7 constant_dynamic-slice_fusion.2
  68.6 0.8 fusion.44
  70.2 2.1 %reshape.118 = f32[16,5,16,256]{3,2,1,0:T(8,128)S(1)} reshape(f32[16,5,4096]{2,1,0:T(8,128)} %get-tuple-element.29) | data formatting | bytes 2621440 | tf_op jit(solution)/shard_map/reshape | solution.py:11
  72.2 1.8 %copy.54 = f32[16,16,5,256]{3,1,2,0:T(8,128)} copy(f32[16,16,5,256]{3,0,2,1:T(8,128)S(1)} %bitcast.76) | data formatting | bytes 2621440 | tf_op jit(solution)/shard_map/transpose | solution.py:11
  74.1 8.2 %all-to-all-start = ((f32[16,16,5,256]{3,1,2,0:T(8,128)}), f32[16,16,5,256]{3,1,2,0:T(8,128)S(1)}, u32[]{:S(2)}, u32[]{:S(2)}) async-start(f32[16,16,5,256]{3,1,2,0:T(8,128)} %copy.54), calls=%async_computation | async-start | bytes 2621440 | tf_op jit(solution)/shard_map/all_to_all | solution.py:16
  84.8 18.4 %all-to-all-done = f32[16,16,5,256]{3,1,2,0:T(8,128)S(1)} async-done(((f32[16,16,5,256]{3,1,2,0:T(8,128)}), f32[16,16,5,256]{3,1,2,0:T(8,128)S(1)}, u32[]{:S(2)}, u32[]{:S(2)}) %all-to-all-start) | async-done | bytes 1310752 | tf_op jit(solution)/shard_map/all_to_all | solution.py:16
  103.3 13.6 %all-gather = f32[128,5,256]{2,0,1:T(8,128)S(1)} all-gather(f32[16,5,256]{2,0,1:T(8,128)S(1)} %reduce_sum.92), channel_id=2, replica_groups=mesh['gx'=4,'gy'=4,'gz'=8] {'gz'}, dimensions={0}, use_global_device_ids=true | all-gather | bytes 737280 | tf_op jit(solution)/shard_map/all_gather | solution.py:21
  117.6 3.5 %all-to-all-start.2 = ((f32[16,1,16]{2,1,0:T(1,128)}), f32[16,1,16]{2,1,0:T(1,128)S(1)}, u32[]{:S(2)}, u32[]{:S(2)}) async-start(f32[16,1,16]{2,1,0:T(1,128)} %broadcast_in_dim.39), calls=%async_computation.2 | async-start | bytes 16384 | tf_op jit(solution)/shard_map/all_to_all | solution.py:27
  122.3 12.7 %all-gather.5 = f32[4,16,5]{1,2,0:T(8,128)S(1)} all-gather(f32[1,16,5]{1,2,0:T(8,128)S(1)} %bitcast.83), channel_id=5, replica_groups=mesh['gx'=4,'gy'=4,'gz'=8] {'gx'}, dimensions={0}, use_global_device_ids=true | all-gather | bytes 1600 | tf_op jit(solution)/shard_map/all_gather | solution.py:54
  135.0 12.3 %all-gather.6 = f32[4,16,5]{1,2,0:T(8,128)S(1)} all-gather(f32[1,16,5]{1,2,0:T(8,128)S(1)} %bitcast.84), channel_id=6, replica_groups=mesh['gx'=4,'gy'=4,'gz'=8] {'gy'}, dimensions={0}, use_global_device_ids=true | all-gather | bytes 1600 | tf_op jit(solution)/shard_map/all_gather | solution.py:54
  147.3 0.7 broadcast_in_dim.24
  148.1 3.6 %all-to-all-start.1 = ((f32[4,16,4,256]{3,2,1,0:T(4,128)}), f32[4,16,4,256]{3,2,1,0:T(4,128)S(1)}, u32[]{:S(2)}, u32[]{:S(2)}) async-start(f32[4,16,4,256]{3,2,1,0:T(4,128)} %broadcast_in_dim.24), calls=%async_computation.1 | async-start | bytes 524288 | tf_op jit(solution)/shard_map/all_to_all | solution.py:27
  152.4 10.1 %all-reduce = f32[64]{0:T(128)S(1)} all-reduce(f32[64]{0:T(128)S(1)} %dynamic-update-slice), channel_id=3, replica_groups=mesh['gx'=4,'gy'=4,'gz'=8] {'gx'}, use_global_device_ids=true, to_apply=%add | all-reduce | flops 64 | bytes 512
  162.8 10.9 %all-reduce.1 = f32[64]{0:T(128)S(1)} all-reduce(f32[64]{0:T(128)S(1)} %dynamic-update-slice.1), channel_id=4, replica_groups=mesh['gx'=4,'gy'=4,'gz'=8] {'gy'}, use_global_device_ids=true, to_apply=%add.1 | all-reduce | flops 64 | bytes 512
  174.5 0.7 copy.66
  (140 shorter events, 18.5 us)
Async XLA Ops:
  0.6 1.6 copy-start
  2.2 18.6 %copy-start.3 = (bf16[1024,512]{1,0:T(8,128)(2,1)S(1)}, bf16[1024,512]{1,0:T(8,128)(2,1)}, u32[]{:S(2)}) copy-start(bf16[1024,512]{1,0:T(8,128)(2,1)} %param.20) | copy-start | bytes 3145732
  2.2 18.6 %copy-start.4 = (bf16[512,256]{1,0:T(8,128)(2,1)S(1)}, bf16[512,256]{1,0:T(8,128)(2,1)}, u32[]{:S(2)}) copy-start(bf16[512,256]{1,0:T(8,128)(2,1)} %param.22) | copy-start | bytes 786436
  2.2 18.6 %copy-start.5 = (f32[1024]{0:T(1024)S(1)}, f32[1024]{0:T(1024)}, u32[]{:S(2)}) copy-start(f32[1024]{0:T(1024)} %param.19) | copy-start | bytes 12292
  2.2 18.6 %copy-start.6 = (f32[512]{0:T(512)S(1)}, f32[512]{0:T(512)}, u32[]{:S(2)}) copy-start(f32[512]{0:T(512)} %param.21) | copy-start | bytes 6148
  2.3 18.6 %copy-start.7 = (f32[256]{0:T(256)S(1)}, f32[256]{0:T(256)}, u32[]{:S(2)}) copy-start(f32[256]{0:T(256)} %param.23) | copy-start | bytes 3076
  20.9 10.5 %copy-start.2 = (bf16[256,1]{0,1:T(2,128)(2,1)S(1)}, bf16[256,1]{0,1:T(2,128)(2,1)}, u32[]{:S(2)}) copy-start(bf16[256,1]{0,1:T(2,128)(2,1)} %param.24) | copy-start | bytes 1540
  20.9 12.8 %copy-start.1 = (s32[16,256]{1,0:T(8,128)S(1)}, s32[16,256]{1,0:T(8,128)}, u32[]{:S(2)}) copy-start(s32[16,256]{1,0:T(8,128)} %param.27) | copy-start | bytes 49156
  70.2 12.1 %copy-start.9 = (u32[128]{0:T(128)S(1)}, u32[128]{0:T(128)}, u32[]{:S(2)}) copy-start(u32[128]{0:T(128)} %constant.49) | copy-start | bytes 1540
  70.2 12.7 %copy-start.8 = (u32[128]{0:T(128)S(1)}, u32[128]{0:T(128)}, u32[]{:S(2)}) copy-start(u32[128]{0:T(128)} %constant.54) | copy-start | bytes 1540
  74.1 29.1 %all-to-all-start = ((f32[16,16,5,256]{3,1,2,0:T(8,128)}), f32[16,16,5,256]{3,1,2,0:T(8,128)S(1)}, u32[]{:S(2)}, u32[]{:S(2)}) async-start(f32[16,16,5,256]{3,1,2,0:T(8,128)} %copy.54), calls=%async_computation | async-start | bytes 2621440 | tf_op jit(solution)/shard_map/all_to_all | solution.py:16
  117.6 29.7 %all-to-all-start.2 = ((f32[16,1,16]{2,1,0:T(1,128)}), f32[16,1,16]{2,1,0:T(1,128)S(1)}, u32[]{:S(2)}, u32[]{:S(2)}) async-start(f32[16,1,16]{2,1,0:T(1,128)} %broadcast_in_dim.39), calls=%async_computation.2 | async-start | bytes 16384 | tf_op jit(solution)/shard_map/all_to_all | solution.py:27
  148.1 26.4 %all-to-all-start.1 = ((f32[4,16,4,256]{3,2,1,0:T(4,128)}), f32[4,16,4,256]{3,2,1,0:T(4,128)S(1)}, u32[]{:S(2)}, u32[]{:S(2)}) async-start(f32[4,16,4,256]{3,2,1,0:T(4,128)} %broadcast_in_dim.24), calls=%async_computation.1 | async-start | bytes 524288 | tf_op jit(solution)/shard_map/all_to_all | solution.py:27
